TPU v7x, 32 devices: a whole 2x2x4 slice. The times are simulated.
32 devices in a mesh: frame: 4 (over y, core), row: 8 (over z, x).
Axes of the slice: x: 2, y: 2, z: 4, core: 2. Of those that a mesh axis runs over, the one named last changes fastest.
Arguments:
- features: float32 [4, 32, 256, 256], P('frame', 'row'), may hold values from -6 to 6
- conv_weight: float32 [2, 3, 3, 256, 256], replicated, may hold values from -0.125 to 0.125
Outputs:
- activations: float32 [4, 32, 256, 256], P('frame', 'row')
All inputs are finite; a program needn't handle non-finite values.
Results may differ from a plain program's by a relative error of at most 0.0001.
Values sent between devices are 32-bit elements; how exact they have to be, the bound alone decides.
A program may use at most 64 MiB of HBM per device.

v0:
```python
import functools

import jax
import jax.numpy as jnp
from jax import lax
from jax.experimental import pallas as pl
from jax.experimental.pallas import tpu as pltpu
from jax.sharding import PartitionSpec as P

MESH = pl.DeviceIdType.MESH
LANES = 128
PAD = 8


def split(value):
    high = value.astype(jnp.bfloat16)
    low = (value - high.astype(jnp.float32)).astype(jnp.bfloat16)
    return high, low


def kernel(
    cuts, x_hbm, w_hbm, out, xin, wbuf, w3, sx, acc, mid, halo, edge, pack, got,
    load_sem, row_send, row_recv, frame_send, frame_recv,
):
    rows, cols, chans = xin.shape
    layers = wbuf.shape[0]
    fold = chans // 8
    last = rows - 1
    frames, bands = lax.axis_size("frame"), lax.axis_size("row")
    t, r = lax.axis_index("frame"), lax.axis_index("row")
    has_row = (r > 0, r < bands - 1)
    has_frame = (t > 0, t < frames - 1)
    row_to = (r - 1, r + 1)
    frame_to = (t - 1, t + 1)

    load_x = pltpu.make_async_copy(x_hbm.at[0], xin, load_sem.at[layers])
    load_x.start()
    load_w = [pltpu.make_async_copy(w_hbm.at[n], wbuf.at[n], load_sem.at[n]) for n in range(layers)]
    for load in load_w:
        load.start()

    barrier = pltpu.get_barrier_semaphore()
    count = 0
    for have, axis, peers in ((has_row, "row", row_to), (has_frame, "frame", frame_to)):
        for side in range(2):
            count = count + have[side].astype(jnp.int32)

            @pl.when(have[side])
            def _():
                pl.semaphore_signal(barrier, inc=1, device_id={axis: peers[side]}, device_id_type=MESH)

    pl.semaphore_wait(barrier, count)

    def maps(layer):
        return xin if layer == 0 else mid.at[layer - 1]

    def span(layer, chunk):
        return cuts[layer][chunk], cuts[layer][chunk + 1] - cuts[layer][chunk]

    def row_copy(layer, side, tile, chunk):
        start, size = span(layer, chunk)
        row = 0 if side == 0 else last
        if tile == 1:
            source = maps(layer).at[row, pl.ds(start, size), pl.ds(LANES, LANES)]
        else:
            source = edge.at[layer, side, pl.ds(start, size)]
        return pltpu.make_async_remote_copy(
            src_ref=source,
            dst_ref=halo.at[layer, 1 - side, tile, pl.ds(start, size)],
            send_sem=row_send.at[layer, side, tile, chunk],
            recv_sem=row_recv.at[layer, side, tile, chunk],
            device_id={"row": row_to[side]},
            device_id_type=MESH,
        )

    def frame_copy(layer, side, chunk):
        start, size = span(layer, chunk)
        return pltpu.make_async_remote_copy(
            src_ref=pack.at[layer, side, pl.ds(start, size)],
            dst_ref=got.at[layer, side, pl.ds(start, size)],
            send_sem=frame_send.at[layer, side, chunk],
            recv_sem=frame_recv.at[layer, side, chunk],
            device_id={"frame": frame_to[side]},
            device_id_type=MESH,
        )

    def send_rows(layer, tile, chunk):
        for side in range(2):

            @pl.when(has_row[side])
            def _():
                row_copy(layer, side, tile, chunk).start()

    def send_frames(layer, chunk):
        start, size = span(layer, chunk)
        lane = lax.broadcasted_iota(jnp.int32, (size, LANES), 1)
        for side in range(2):
            full = jnp.zeros((size, LANES), jnp.float32)
            for row in range(rows):
                value = maps(layer)[row, pl.ds(start, size), pl.ds(0, LANES)]
                shift = ((row - side) * fold) % LANES
                value = pltpu.roll(value, shift, 1) if shift else value
                full = jnp.where(lane // fold == row, value, full)
            pack[layer, side, pl.ds(start, size)] = full

            @pl.when(has_frame[side])
            def _():
                frame_copy(layer, side, chunk).start()

    def take_frames(layer, chunk):
        start, size = span(layer, chunk)
        for side in range(2):

            @pl.when(has_frame[1 - side])
            def _():
                frame_copy(layer, side, chunk).wait_recv()

            @pl.when(jnp.logical_not(has_frame[1 - side]))
            def _():
                got[layer, side, pl.ds(start, size)] = jnp.zeros((size, LANES), jnp.float32)

    def shifted_tile(layer, chunk, row):
        start, size = span(layer, chunk)
        lane = lax.broadcasted_iota(jnp.int32, (size, LANES), 1)
        value = maps(layer)[row, pl.ds(start, size), pl.ds(0, LANES)]
        for side in range(2):
            part = got[layer, side, pl.ds(start, size)]
            shift = ((side - row) * fold) % LANES
            part = pltpu.roll(part, shift, 1) if shift else part
            value = jnp.where(lane // fold == side, part, value)
        return value

    def put(row, start, size, tile, value):
        high, low = split(value)
        sx[row, pl.ds(start, size), pl.ds(tile * LANES, LANES)] = high
        sx[row, pl.ds(start, size), pl.ds(chans + tile * LANES, LANES)] = low
        sx[row, pl.ds(start, size), pl.ds(2 * chans + tile * LANES, LANES)] = high

    def lower_edges(layer, chunk):
        start, size = span(layer, chunk)
        for row in range(rows):
            value = shifted_tile(layer, chunk, row)
            if row == 0:
                edge[layer, 0, pl.ds(start, size)] = value
            if row == last:
                edge[layer, 1, pl.ds(start, size)] = value
        send_rows(layer, 0, chunk)

    def fill(layer):
        for chunk in range(len(cuts[layer]) - 1):
            start, size = span(layer, chunk)
            for row in range(rows):
                put(row + 1, start, size, 0, shifted_tile(layer, chunk, row))
                put(row + 1, start, size, 1, maps(layer)[row, pl.ds(start, size), pl.ds(LANES, LANES)])
        blank = jnp.zeros((cols, 3 * chans), jnp.bfloat16)
        sx[0] = blank
        sx[rows + 1] = blank

    def split_weights(layer):
        load_w[layer].wait()

        def tap(index, carry):
            down, across = index // 3, index % 3
            high, low = split(wbuf[layer, down, across])
            base = pl.multiple_of(down * 3 * chans, 3 * chans)
            w3[layer, across, pl.ds(base, chans)] = high
            w3[layer, across, pl.ds(base + chans, chans)] = high
            w3[layer, across, pl.ds(base + 2 * chans, chans)] = low
            return carry

        lax.fori_loop(0, 9, tap, 0)

    def inner(layer):
        def across(tap, carry):
            for first, count, low, high in ((0, 1, 1, 3), (1, rows - 2, 0, 3), (last, 1, 0, 2)):
                left = jnp.concatenate(
                    [
                        sx[pl.ds(first + down, count)].reshape(count * cols, 3 * chans)
                        for down in range(low, high)
                    ],
                    axis=1,
                )
                taps = w3[layer, tap, pl.ds(low * 3 * chans, (high - low) * 3 * chans)]
                total = jnp.dot(left, taps, preferred_element_type=jnp.float32)
                acc[tap, pl.ds(first, count), pl.ds(PAD, cols)] = total.reshape(count, cols, chans)
            return carry

        lax.fori_loop(0, 3, across, 0)

    def finish(row, start, size):
        total = acc[0, row, pl.ds(PAD + start - 1, size)] + acc[1, row, pl.ds(PAD + start, size)]
        total = total + acc[2, row, pl.ds(PAD + start + 1, size)]
        return jnp.maximum(total, 0.0)

    def outer(layer, chunk):
        start, size = span(layer, chunk)
        for side in range(2):
            place = 0 if side == 0 else rows + 1

            @pl.when(has_row[side])
            def _():
                for tile in range(2):
                    row_copy(layer, 1 - side, tile, chunk).wait_recv()
                for tile in range(2):
                    put(place, start, size, tile, halo[layer, side, tile, pl.ds(start, size)])

        def across(tap, carry):
            for place, row, down in ((0, 0, 0), (rows + 1, last, 2)):
                extra = jnp.dot(
                    sx[place, pl.ds(start, size)],
                    w3[layer, tap, pl.ds(down * 3 * chans, 3 * chans)],
                    preferred_element_type=jnp.float32,
                )
                acc[tap, row, pl.ds(PAD + start, size)] += extra
            return carry

        lax.fori_loop(0, 3, across, 0)

    chunks = len(cuts[0]) - 1
    load_x.wait()
    send_rows(0, 1, 0)
    for chunk in range(chunks):
        send_frames(0, chunk)
    split_weights(0)
    acc[:, :, pl.ds(0, PAD)] = jnp.zeros((3, rows, PAD, chans), jnp.float32)
    acc[:, :, pl.ds(PAD + cols, PAD)] = jnp.zeros((3, rows, PAD, chans), jnp.float32)
    for chunk in range(chunks):
        if chunk > 0:
            send_rows(0, 1, chunk)
        take_frames(0, chunk)
        lower_edges(0, chunk)
    for layer in range(layers):
        final = layer == layers - 1
        fill(layer)
        inner(layer)
        target = out if final else mid.at[layer]
        for row in range(1, last):
            target[row] = finish(row, 0, cols)
        for chunk in range(chunks):
            outer(layer, chunk)
            start = cuts[layer + 1][chunk]
            size = cuts[layer + 1][chunk + 1] - start
            for row in (0, last):
                target[row, pl.ds(start, size)] = finish(row, start, size)
            if not final:
                send_rows(layer + 1, 1, chunk)
                send_frames(layer + 1, chunk)
                if chunk == 0:
                    split_weights(layer + 1)
                take_frames(layer + 1, chunk)
                lower_edges(layer + 1, chunk)

    for layer in range(layers):
        for chunk in range(chunks):
            for side in range(2):

                @pl.when(has_row[side])
                def _():
                    for tile in range(2):
                        row_copy(layer, side, tile, chunk).wait_send()

                @pl.when(has_frame[side])
                def _():
                    frame_copy(layer, side, chunk).wait_send()


def store(y_ref, o_hbm, sem):
    copies = [pltpu.make_async_copy(y_ref.at[n], o_hbm.at[0, n], sem.at[n]) for n in range(y_ref.shape[0])]
    for copy in copies:
        copy.start()
    for copy in copies:
        copy.wait()


def local(features, conv_weight):
    _, rows, cols, chans = features.shape
    layers = conv_weight.shape[0]
    half, step = cols // 2, 2 * PAD
    cuts = [[0, half + step * (layers - 1 - n), cols] for n in range(layers)] + [[0, half - step, cols]]
    chunks = len(cuts[0]) - 1
    f32, bf16 = jnp.float32, jnp.bfloat16
    dma = pltpu.SemaphoreType.DMA
    result = pl.pallas_call(
        functools.partial(kernel, cuts),
        out_shape=pltpu.VMEM((rows, cols, chans), f32),
        in_specs=[pl.BlockSpec(memory_space=pl.ANY)] * 2,
        out_specs=pl.BlockSpec(memory_space=pltpu.VMEM),
        scratch_shapes=[
            pltpu.VMEM((rows, cols, chans), f32),
            pltpu.VMEM(conv_weight.shape, f32),
            pltpu.VMEM((layers, 3, 9 * chans, chans), bf16),
            pltpu.VMEM((rows + 2, cols, 3 * chans), bf16),
            pltpu.VMEM((3, rows, cols + 2 * PAD, chans), f32),
            pltpu.VMEM((layers - 1, rows, cols, chans), f32),
            pltpu.VMEM((layers, 2, 2, cols, LANES), f32),
            pltpu.VMEM((layers, 2, cols, LANES), f32),
            pltpu.VMEM((layers, 2, cols, LANES), f32),
            pltpu.VMEM((layers, 2, cols, LANES), f32),
            dma((layers + 1,)),
            dma((layers, 2, 2, chunks)),
            dma((layers, 2, 2, chunks)),
            dma((layers, 2, chunks)),
            dma((layers, 2, chunks)),
        ],
        compiler_params=pltpu.CompilerParams(
            collective_id=0, has_side_effects=True, vmem_limit_bytes=62 * 1024 * 1024
        ),
    )(features, conv_weight)
    return pl.pallas_call(
        store,
        out_shape=jax.ShapeDtypeStruct(features.shape, f32),
        in_specs=[pl.BlockSpec(memory_space=pltpu.VMEM)],
        out_specs=pl.BlockSpec(memory_space=pl.ANY),
        scratch_shapes=[dma((rows,))],
        compiler_params=pltpu.CompilerParams(vmem_limit_bytes=2 * 1024 * 1024),
    )(result)


def solution(mesh):
    placed = (P("frame", "row", None, None), P())
    return jax.shard_map(
        local, mesh=mesh, in_specs=placed, out_specs=P("frame", "row", None, None), check_vma=False
    )
```

profile of v0, /device:TPU:25, one launch (start us, length us, event | category | flops | bytes accessed | tf_op | source)
XLA Modules:
  0.0 29.0 jit_solution(17230659430971010677)
XLA Ops:
  0.0 28.0 %shard_map.28.y_ref = f32[4,256,256]{2,1,0:T(8,128)S(1)} custom-call(f32[1,4,256,256]{3,2,1,0:T(8,128)} %x_hbm.1, f32[2,3,3,256,256]{4,3,2,1,0:T(8,128)} %w_hbm.1), custom_call_target="tpu_custom_call" | custom-call | tf_op jit(solution)/shard_map/pallas_call | solution.py:283
  28.0 1.0 %shard_map.29 = f32[1,4,256,256]{3,2,1,0:T(8,128)} custom-call(f32[4,256,256]{2,1,0:T(8,128)S(1)} %shard_map.28.y_ref), custom_call_target="tpu_custom_call" | custom-call | tf_op jit(solution)/shard_map/pallas_call | solution.py:309
where the time goes:
time: 29.2 us; the launch traced here: 29 us
  Pallas kernels  29 us (99%)
    pallas_call x1, Pallas kernels, local(): pl.pallas_call(functools.partial(kernel, cuts), out_shape=pltpu.VMEM((row...  28 us
    pallas_call x1, Pallas kernels, local(): pl.pallas_call(store, out_shape=jax.ShapeDtypeStruct(features.shape, f32)...  1 us

commit v1 on v0

v1 whole, which is shorter than its diff:
```python
import jax
import jax.numpy as jnp
from jax import lax
from jax.experimental import pallas as pl
from jax.experimental.pallas import tpu as pltpu
from jax.sharding import PartitionSpec as P

MESH = pl.DeviceIdType.MESH
LANES = 128
PAD = 8
FAR, NEAR = 0, 1


def split(value):
    high = value.astype(jnp.bfloat16)
    low = (value - high.astype(jnp.float32)).astype(jnp.bfloat16)
    return high, low


def kernel(
    x_hbm, w_hbm, out, xin, wbuf, w3, sx, acc, mid, pack, got, half, hmain, hhalf, hshift,
    load_x, load_w, row_send, row_recv, frame_send, frame_recv,
):
    rows, cols, chans = xin.shape
    layers = wbuf.shape[0]
    fold = chans // 8
    last = rows - 1
    groups = LANES // fold
    part = cols // groups
    rest = LANES - 2 * fold
    halves = LANES // rest
    frames, bands = lax.axis_size("frame"), lax.axis_size("row")
    t, r = lax.axis_index("frame"), lax.axis_index("row")
    turned = r % 2
    sign = 1 - 2 * turned
    row_to = (r - sign, r + sign)
    has_row = tuple((peer >= 0) & (peer < bands) for peer in row_to)
    edge = (0, last)
    has_frame = (t > 0, t < frames - 1)
    frame_to = (t - 1, t + 1)

    def place(row, count):
        return row + turned * (count - 1 - 2 * row)

    loads_x = [pltpu.make_async_copy(x_hbm.at[0, place(q, rows)], xin.at[q], load_x.at[q]) for q in range(rows)]
    loads_w = [
        [pltpu.make_async_copy(w_hbm.at[n, place(d, 3)], wbuf.at[n, d], load_w.at[n, d]) for d in range(3)]
        for n in range(layers)
    ]
    for load in loads_x:
        load.start()
    for per_layer in loads_w:
        for load in per_layer:
            load.start()

    barrier = pltpu.get_barrier_semaphore()
    count = 0
    for have, axis, peers in ((has_row, "row", row_to), (has_frame, "frame", frame_to)):
        for side in range(2):
            count = count + have[side].astype(jnp.int32)

            @pl.when(have[side])
            def _():
                pl.semaphore_signal(barrier, inc=1, device_id={axis: peers[side]}, device_id_type=MESH)

    def maps(layer):
        return xin if layer == 0 else mid.at[layer - 1]

    def row_copy(layer, kind, piece):
        if piece == 0:
            source = maps(layer).at[edge[kind], :, pl.ds(LANES, chans - LANES)]
            target = hmain.at[layer, kind]
        elif piece == 1:
            source, target = half.at[layer, kind], hhalf.at[layer, kind]
        else:
            source = got.at[layer, piece - 2, edge[kind]]
            target = hshift.at[layer, kind, piece - 2]
        return pltpu.make_async_remote_copy(
            src_ref=source,
            dst_ref=target,
            send_sem=row_send.at[layer, kind, piece],
            recv_sem=row_recv.at[layer, kind, piece],
            device_id={"row": row_to[kind]},
            device_id_type=MESH,
        )

    def sent(kind, piece):
        return has_row[kind] if piece < 2 else has_row[kind] & has_frame[3 - piece]

    def each_piece(layer, kind, pieces, action):
        for piece in pieces:

            @pl.when(sent(kind, piece))
            def _():
                getattr(row_copy(layer, kind, piece), action)()

    def blocks(layer):
        return ((0, rows),) if layer == 0 else ((0, 1), (1, rows - 2), (last, 1))

    def frame_copy(layer, side, block):
        start, size = blocks(layer)[block]
        return pltpu.make_async_remote_copy(
            src_ref=pack.at[layer, side, pl.ds(start, size)],
            dst_ref=got.at[layer, side, pl.ds(start, size)],
            send_sem=frame_send.at[layer, side, block],
            recv_sem=frame_recv.at[layer, side, block],
            device_id={"frame": frame_to[side]},
            device_id_type=MESH,
        )

    def pack_frames(layer, block):
        start, size = blocks(layer)[block]
        lane = lax.broadcasted_iota(jnp.int32, (part, LANES), 1)
        for side in range(2):
            for row in range(start, start + size):
                full = None
                for group in range(groups):
                    value = maps(layer)[row, pl.ds(group * part, part), pl.ds(0, LANES)]
                    shift = ((group - side) * fold) % LANES
                    value = pltpu.roll(value, shift, 1) if shift else value
                    full = value if full is None else jnp.where(lane // fold == group, value, full)
                pack[layer, side, row] = full

    def send_frames(layer, block):
        for side in range(2):

            @pl.when(has_frame[side])
            def _():
                frame_copy(layer, side, block).start()

    def take_frames(layer, block):
        for side in range(2):

            @pl.when(has_frame[1 - side])
            def _():
                frame_copy(layer, side, block).wait_recv()

    def pack_half(layer, kind):
        size = cols // halves
        lane = lax.broadcasted_iota(jnp.int32, (size, LANES), 1)
        full = None
        for group in range(halves):
            value = maps(layer)[edge[kind], pl.ds(group * size, size), pl.ds(0, LANES)]
            shift = (group * rest - 2 * fold) % LANES
            value = pltpu.roll(value, shift, 1) if shift else value
            full = value if full is None else jnp.where(lane // rest == group, value, full)
        half[layer, kind] = full

    def put(spot, start, size, tile, value):
        high, low = split(value)
        sx[spot, pl.ds(start, size), pl.ds(tile, value.shape[1])] = high
        sx[spot, pl.ds(start, size), pl.ds(chans + tile, value.shape[1])] = low
        sx[spot, pl.ds(start, size), pl.ds(2 * chans + tile, value.shape[1])] = high

    def put_lower(spot, rest_of, shifted):
        lane = lax.broadcasted_iota(jnp.int32, (part, LANES), 1)
        for group in range(groups):
            value = rest_of(group * part)
            for side in range(2):
                moved = shifted(side)
                shift = ((side - group) * fold) % LANES
                moved = pltpu.roll(moved, shift, 1) if shift else moved
                value = jnp.where(lane // fold == side, moved, value)
            put(spot, group * part, part, 0, value)

    def put_row(layer, row):
        put_lower(
            row + 1,
            lambda start: maps(layer)[row, pl.ds(start, part), pl.ds(0, LANES)],
            lambda side: got[layer, side, row],
        )
        put(row + 1, 0, cols, LANES, maps(layer)[row, :, pl.ds(LANES, chans - LANES)])

    def put_halo(layer, kind):
        spot = 0 if kind == FAR else rows + 1
        size = cols // halves

        def rest_of(start):
            group = start // size
            value = hhalf[layer, kind, pl.ds(start - group * size, part)]
            shift = (2 * fold - group * rest) % LANES
            return pltpu.roll(value, shift, 1) if shift else value

        put_lower(spot, rest_of, lambda side: hshift[layer, kind, side])
        put(spot, 0, cols, LANES, hmain[layer, kind])

    def split_weights(layer):
        for load in loads_w[layer]:
            load.wait()

        def tap(index, carry):
            down, across = index // 3, index % 3
            high, low = split(wbuf[layer, down, across])
            base = pl.multiple_of(down * 3 * chans, 3 * chans)
            w3[layer, across, pl.ds(base, chans)] = high
            w3[layer, across, pl.ds(base + chans, chans)] = high
            w3[layer, across, pl.ds(base + 2 * chans, chans)] = low
            return carry

        lax.fori_loop(0, 9, tap, 0)

    def inner(layer, parts, first_tap, taps):
        def across(tap, carry):
            for first, count, low, high, add in parts:
                left = jnp.concatenate(
                    [
                        sx[pl.ds(first + down, count)].reshape(count * cols, 3 * chans)
                        for down in range(low, high)
                    ],
                    axis=1,
                )
                right = w3[layer, tap, pl.ds(low * 3 * chans, (high - low) * 3 * chans)]
                total = jnp.dot(left, right, preferred_element_type=jnp.float32)
                total = total.reshape(count, cols, chans)
                if add:
                    acc[tap, pl.ds(first, count), pl.ds(PAD, cols)] += total
                else:
                    acc[tap, pl.ds(first, count), pl.ds(PAD, cols)] = total
            return carry

        lax.fori_loop(first_tap, first_tap + taps, across, 0)

    whole_parts = ((0, 1, 1, 3, False), (1, rows - 2, 0, 3, False), (last, 1, 0, 2, False))
    early_parts = ((0, 1, 2, 3, False), (1, 1, 1, 3, False), (2, rows - 3, 0, 3, False), (last, 1, 0, 2, False))
    late_parts = ((0, 1, 1, 2, True), (1, 1, 0, 1, True))

    def outer(layer, kind):
        @pl.when(has_row[kind])
        def _():
            each_piece(layer, kind, range(4), "wait_recv")
            put_halo(layer, kind)

        inner(layer, ((0, 1, 0, 1, True),) if kind == FAR else ((last, 1, 2, 3, True),), 0, 3)

    def finish(layer, row):
        total = acc[0, row, pl.ds(PAD - 1, cols)] + acc[1, row, pl.ds(PAD, cols)]
        total = jnp.maximum(total + acc[2, row, pl.ds(PAD + 1, cols)], 0.0)
        if layer == layers - 1:
            out[place(row, rows)] = total
        else:
            mid[layer, row] = total

    def blank():
        acc[:, :, pl.ds(0, PAD)] = jnp.zeros((3, rows, PAD, chans), jnp.float32)
        acc[:, :, pl.ds(PAD + cols, PAD)] = jnp.zeros((3, rows, PAD, chans), jnp.float32)
        for kind, spot in ((FAR, 0), (NEAR, rows + 1)):

            @pl.when(jnp.logical_not(has_row[kind]))
            def _():
                sx[spot] = jnp.zeros((cols, 3 * chans), jnp.bfloat16)

        for side in range(2):

            @pl.when(jnp.logical_not(has_frame[1 - side]))
            def _():
                for layer in range(layers):
                    got[layer, side] = jnp.zeros((rows, part, LANES), jnp.float32)
                    for kind in range(2):
                        hshift[layer, kind, side] = jnp.zeros((part, LANES), jnp.float32)

    for load in loads_x:
        load.wait()
    pack_frames(0, 0)
    pack_half(0, NEAR)
    pack_half(0, FAR)
    blank()
    pl.semaphore_wait(barrier, count)
    send_frames(0, 0)
    each_piece(0, NEAR, range(2), "start")
    split_weights(0)
    take_frames(0, 0)
    each_piece(0, NEAR, range(2, 4), "start")
    for row in range(rows):
        put_row(0, row)
    inner(0, whole_parts, 0, 1)
    each_piece(0, FAR, range(4), "start")
    inner(0, whole_parts, 1, 2)
    for layer in range(layers):
        final = layer == layers - 1
        outer(layer, NEAR)
        finish(layer, last)
        if not final:
            each_piece(layer + 1, NEAR, range(1), "start")
            pack_frames(layer + 1, 2)
            send_frames(layer + 1, 2)
            pack_half(layer + 1, NEAR)
            each_piece(layer + 1, NEAR, range(1, 2), "start")
        for row in range(1, last):
            finish(layer, row)
        if not final:
            pack_frames(layer + 1, 1)
            send_frames(layer + 1, 1)
            split_weights(layer + 1)
            take_frames(layer + 1, 2)
            each_piece(layer + 1, NEAR, range(2, 4), "start")
            put_row(layer + 1, last)
            take_frames(layer + 1, 1)
            for row in range(1, last):
                put_row(layer + 1, row)
        outer(layer, FAR)
        finish(layer, 0)
        if not final:
            each_piece(layer + 1, FAR, range(1), "start")
            pack_frames(layer + 1, 0)
            send_frames(layer + 1, 0)
            pack_half(layer + 1, FAR)
            each_piece(layer + 1, FAR, range(1, 2), "start")
            inner(layer + 1, early_parts, 0, 1)
            take_frames(layer + 1, 0)
            each_piece(layer + 1, FAR, range(2, 4), "start")
            inner(layer + 1, early_parts, 1, 2)
            put_row(layer + 1, 0)
            inner(layer + 1, late_parts, 0, 3)

    for layer in range(layers):
        for kind in range(2):
            each_piece(layer, kind, range(4), "wait_send")
        for side in range(2):
            for block in range(len(blocks(layer))):

                @pl.when(has_frame[side])
                def _():
                    frame_copy(layer, side, block).wait_send()


def store(y_ref, o_hbm, sem):
    copies = [pltpu.make_async_copy(y_ref.at[n], o_hbm.at[0, n], sem.at[n]) for n in range(y_ref.shape[0])]
    for copy in copies:
        copy.start()
    for copy in copies:
        copy.wait()


def local(features, conv_weight):
    _, rows, cols, chans = features.shape
    layers = conv_weight.shape[0]
    fold = chans // 8
    part = cols // (LANES // fold)
    halved = cols // (LANES // (LANES - 2 * fold))
    f32, bf16 = jnp.float32, jnp.bfloat16
    dma = pltpu.SemaphoreType.DMA
    result = pl.pallas_call(
        kernel,
        out_shape=pltpu.VMEM((rows, cols, chans), f32),
        in_specs=[pl.BlockSpec(memory_space=pl.ANY)] * 2,
        out_specs=pl.BlockSpec(memory_space=pltpu.VMEM),
        scratch_shapes=[
            pltpu.VMEM((rows, cols, chans), f32),
            pltpu.VMEM(conv_weight.shape, f32),
            pltpu.VMEM((layers, 3, 9 * chans, chans), bf16),
            pltpu.VMEM((rows + 2, cols, 3 * chans), bf16),
            pltpu.VMEM((3, rows, cols + 2 * PAD, chans), f32),
            pltpu.VMEM((layers - 1, rows, cols, chans), f32),
            pltpu.VMEM((layers, 2, rows, part, LANES), f32),
            pltpu.VMEM((layers, 2, rows, part, LANES), f32),
            pltpu.VMEM((layers, 2, halved, LANES), f32),
            pltpu.VMEM((layers, 2, cols, chans - LANES), f32),
            pltpu.VMEM((layers, 2, halved, LANES), f32),
            pltpu.VMEM((layers, 2, 2, part, LANES), f32),
            dma((rows,)),
            dma((layers, 3)),
            dma((layers, 2, 4)),
            dma((layers, 2, 4)),
            dma((layers, 2, 3)),
            dma((layers, 2, 3)),
        ],
        compiler_params=pltpu.CompilerParams(
            collective_id=0, has_side_effects=True, vmem_limit_bytes=62 * 1024 * 1024
        ),
    )(features, conv_weight)
    return pl.pallas_call(
        store,
        out_shape=jax.ShapeDtypeStruct(features.shape, f32),
        in_specs=[pl.BlockSpec(memory_space=pltpu.VMEM)],
        out_specs=pl.BlockSpec(memory_space=pl.ANY),
        scratch_shapes=[dma((rows,))],
        compiler_params=pltpu.CompilerParams(vmem_limit_bytes=2 * 1024 * 1024),
    )(result)


def solution(mesh):
    placed = (P("frame", "row", None, None), P())
    return jax.shard_map(
        local, mesh=mesh, in_specs=placed, out_specs=P("frame", "row", None, None), check_vma=False
    )
```

time: 29.2 us -> 32.5 us (1.11)
  the two profiles are of different devices: /device:TPU:25 before, /device:TPU:17 now
where the time goes in v1:
time: 32.5 us; the launch traced here: 32.4 us
  Pallas kernels  32.4 us (100%)
    pallas_call x1, Pallas kernels, local(): pl.pallas_call(kernel, out_shape=pltpu.VMEM((rows, cols, chans), f32), in...  31.4 us
    pallas_call x1, Pallas kernels, local(): pl.pallas_call(store, out_shape=jax.ShapeDtypeStruct(features.shape, f32)...  1 us

profile of v1, /device:TPU:17, one launch (start us, length us, event | category | flops | bytes accessed | tf_op | source)
XLA Modules:
  0.0 32.4 jit_solution(14188239446291432944)
XLA Ops:
  0.0 31.4 %shard_map.28.y_ref = f32[4,256,256]{2,1,0:T(8,128)S(1)} custom-call(f32[1,4,256,256]{3,2,1,0:T(8,128)} %x_hbm.1, f32[2,3,3,256,256]{4,3,2,1,0:T(8,128)} %w_hbm.1), custom_call_target="tpu_custom_call" | custom-call | tf_op jit(solution)/shard_map/pallas_call | solution.py:342
  31.4 1.0 %shard_map.29 = f32[1,4,256,256]{3,2,1,0:T(8,128)} custom-call(f32[4,256,256]{2,1,0:T(8,128)S(1)} %shard_map.28.y_ref), custom_call_target="tpu_custom_call" | custom-call | tf_op jit(solution)/shard_map/pallas_call | solution.py:371

commit v2 on v1

--- a/solution.py
+++ b/solution.py
@@ -18,11 +18,13 @@
 
 
 def kernel(
-    x_hbm, w_hbm, out, xin, wbuf, w3, sx, acc, mid, pack, got, half, hmain, hhalf, hshift,
-    load_x, load_w, row_send, row_recv, frame_send, frame_recv,
+    x_hbm, w_hbm, out, xin, wbuf, w3, sx, acc, mid, pack, got, half, hmain, hhalf, hshift, rmain, rhalf,
+    load_x, load_w, row_send, row_recv, frame_send, frame_recv, relay_send, relay_recv,
 ):
     rows, cols, chans = xin.shape
     layers = wbuf.shape[0]
+    tiles = chans // LANES
+    both = range(tiles)
     fold = chans // 8
     last = rows - 1
     groups = LANES // fold
@@ -39,6 +41,28 @@
     has_frame = (t > 0, t < frames - 1)
     frame_to = (t - 1, t + 1)
 
+    pairs = bands // 2
+
+    def shared(place):
+        step = place // 2
+        return 4 * (step + (place % 2) * (pairs - 1 - 2 * step)) // pairs
+
+    def takes(place, piece):
+        quarters = shared(place)
+        return quarters >= 2 if piece == 0 else quarters % 2 == 1
+
+    def within(place):
+        return (place >= 0) & (place < bands)
+
+    def relayed(piece):
+        return has_row[FAR] & has_row[NEAR] & takes(r, piece)
+
+    onward = r + 2 * sign
+    behind = r - 2 * sign
+
+    def relays(piece):
+        return has_row[NEAR] & within(onward) & takes(row_to[NEAR], piece)
+
     def place(row, count):
         return row + turned * (count - 1 - 2 * row)
 
@@ -49,9 +73,6 @@
     ]
     for load in loads_x:
         load.start()
-    for per_layer in loads_w:
-        for load in per_layer:
-            load.start()
 
     barrier = pltpu.get_barrier_semaphore()
     count = 0
@@ -63,12 +84,23 @@
             def _():
                 pl.semaphore_signal(barrier, inc=1, device_id={axis: peers[side]}, device_id_type=MESH)
 
+    for peer in (onward, behind):
+        count = count + within(peer).astype(jnp.int32)
+
+        @pl.when(within(peer))
+        def _():
+            pl.semaphore_signal(barrier, inc=1, device_id={"row": peer}, device_id_type=MESH)
+
     def maps(layer):
         return xin if layer == 0 else mid.at[layer - 1]
 
-    def row_copy(layer, kind, piece):
+    def row_copy(layer, kind, piece, relay=False):
         if piece == 0:
-            source = maps(layer).at[edge[kind], :, pl.ds(LANES, chans - LANES)]
+            upper = pl.ds(LANES, chans - LANES)
+            if layer == 0:
+                source = x_hbm.at[0, place(edge[kind], rows), :, upper]
+            else:
+                source = maps(layer).at[edge[kind], :, upper]
             target = hmain.at[layer, kind]
         elif piece == 1:
             source, target = half.at[layer, kind], hhalf.at[layer, kind]
@@ -77,13 +109,38 @@
             target = hshift.at[layer, kind, piece - 2]
         return pltpu.make_async_remote_copy(
             src_ref=source,
-            dst_ref=target,
+            dst_ref=(rmain, rhalf)[piece].at[layer] if relay else target,
             send_sem=row_send.at[layer, kind, piece],
-            recv_sem=row_recv.at[layer, kind, piece],
-            device_id={"row": row_to[kind]},
+            recv_sem=relay_recv.at[layer, piece] if relay else row_recv.at[layer, kind, piece],
+            device_id={"row": row_to[NEAR if relay else kind]},
             device_id_type=MESH,
         )
 
+    def relay_copy(layer, piece):
+        return pltpu.make_async_remote_copy(
+            src_ref=(rmain, rhalf)[piece].at[layer],
+            dst_ref=(hmain, hhalf)[piece].at[layer, FAR],
+            send_sem=relay_send.at[layer, piece],
+            recv_sem=row_recv.at[layer, FAR, piece],
+            device_id={"row": onward},
+            device_id_type=MESH,
+        )
+
+    def start_far(layer, piece):
+        @pl.when(relayed(piece))
+        def _():
+            row_copy(layer, FAR, piece, True).start()
+
+        @pl.when(has_row[FAR] & jnp.logical_not(relayed(piece)))
+        def _():
+            row_copy(layer, FAR, piece).start()
+
+    def forward(layer, piece):
+        @pl.when(relays(piece))
+        def _():
+            row_copy(layer, FAR, piece, True).wait_recv()
+            relay_copy(layer, piece).start()
+
     def sent(kind, piece):
         return has_row[kind] if piece < 2 else has_row[kind] & has_frame[3 - piece]
 
@@ -94,11 +151,10 @@
             def _():
                 getattr(row_copy(layer, kind, piece), action)()
 
-    def blocks(layer):
-        return ((0, rows),) if layer == 0 else ((0, 1), (1, rows - 2), (last, 1))
+    blocks = ((0, 1), (1, rows - 2), (last, 1))
 
     def frame_copy(layer, side, block):
-        start, size = blocks(layer)[block]
+        start, size = blocks[block]
         return pltpu.make_async_remote_copy(
             src_ref=pack.at[layer, side, pl.ds(start, size)],
             dst_ref=got.at[layer, side, pl.ds(start, size)],
@@ -109,7 +165,7 @@
         )
 
     def pack_frames(layer, block):
-        start, size = blocks(layer)[block]
+        start, size = blocks[block]
         lane = lax.broadcasted_iota(jnp.int32, (part, LANES), 1)
         for side in range(2):
             for row in range(start, start + size):
@@ -148,9 +204,12 @@
 
     def put(spot, start, size, tile, value):
         high, low = split(value)
-        sx[spot, pl.ds(start, size), pl.ds(tile, value.shape[1])] = high
-        sx[spot, pl.ds(start, size), pl.ds(chans + tile, value.shape[1])] = low
-        sx[spot, pl.ds(start, size), pl.ds(2 * chans + tile, value.shape[1])] = high
+        for n, piece in enumerate((high, low, high)):
+            sx[spot, pl.ds(start, size), pl.ds((3 * tile + n) * LANES, LANES)] = piece
+
+    def put_upper(spot, source):
+        for tile in range(1, tiles):
+            put(spot, 0, cols, tile, source[:, pl.ds((tile - 1) * LANES, LANES)])
 
     def put_lower(spot, rest_of, shifted):
         lane = lax.broadcasted_iota(jnp.int32, (part, LANES), 1)
@@ -163,13 +222,15 @@
                 value = jnp.where(lane // fold == side, moved, value)
             put(spot, group * part, part, 0, value)
 
-    def put_row(layer, row):
+    def put_row_upper(layer, row):
+        put_upper(row + 1, maps(layer).at[row, :, pl.ds(LANES, chans - LANES)])
+
+    def put_row_lower(layer, row):
         put_lower(
             row + 1,
             lambda start: maps(layer)[row, pl.ds(start, part), pl.ds(0, LANES)],
             lambda side: got[layer, side, row],
         )
-        put(row + 1, 0, cols, LANES, maps(layer)[row, :, pl.ds(LANES, chans - LANES)])
 
     def put_halo(layer, kind):
         spot = 0 if kind == FAR else rows + 1
@@ -182,7 +243,7 @@
             return pltpu.roll(value, shift, 1) if shift else value
 
         put_lower(spot, rest_of, lambda side: hshift[layer, kind, side])
-        put(spot, 0, cols, LANES, hmain[layer, kind])
+        put_upper(spot, hmain.at[layer, kind])
 
     def split_weights(layer):
         for load in loads_w[layer]:
@@ -191,38 +252,57 @@
         def tap(index, carry):
             down, across = index // 3, index % 3
             high, low = split(wbuf[layer, down, across])
-            base = pl.multiple_of(down * 3 * chans, 3 * chans)
-            w3[layer, across, pl.ds(base, chans)] = high
-            w3[layer, across, pl.ds(base + chans, chans)] = high
-            w3[layer, across, pl.ds(base + 2 * chans, chans)] = low
+            for tile in range(tiles):
+                span = slice(tile * LANES, (tile + 1) * LANES)
+                base = pl.multiple_of((3 * tile + down) * 3 * LANES, LANES)
+                for n, piece in enumerate((high, high, low)):
+                    w3[layer, across, pl.ds(base + n * LANES, LANES)] = piece[span]
             return carry
 
         lax.fori_loop(0, 9, tap, 0)
 
-    def inner(layer, parts, first_tap, taps):
+    def parts_of(sources, seen):
+        parts = []
+        for row in range(rows):
+            downs = [down for down in range(3) if row + down - 1 in sources]
+            if downs:
+                key = (downs[0], downs[-1] + 1, row in seen)
+                if parts and parts[-1][2:] == key and sum(parts[-1][:2]) == row:
+                    parts[-1] = (parts[-1][0], parts[-1][1] + 1) + key
+                else:
+                    parts.append((row, 1) + key)
+        seen.update(part[0] + n for part in parts for n in range(part[1]))
+        return parts
+
+    def inner(layer, parts, first_tap, taps, which):
+        deep = 3 * LANES
+
         def across(tap, carry):
             for first, count, low, high, add in parts:
                 left = jnp.concatenate(
                     [
-                        sx[pl.ds(first + down, count)].reshape(count * cols, 3 * chans)
+                        sx[pl.ds(first + down, count), :, pl.ds(tile * deep, deep)].reshape(count * cols, deep)
+                        for tile in which
                         for down in range(low, high)
                     ],
                     axis=1,
                 )
-                right = w3[layer, tap, pl.ds(low * 3 * chans, (high - low) * 3 * chans)]
+                right = jnp.concatenate(
+                    [
+                        w3[layer, tap, pl.ds((3 * tile + low) * deep, (high - low) * deep)]
+                        for tile in which
+                    ],
+                    axis=0,
+                )
                 total = jnp.dot(left, right, preferred_element_type=jnp.float32)
                 total = total.reshape(count, cols, chans)
                 if add:
-                    acc[tap, pl.ds(first, count), pl.ds(PAD, cols)] += total
+                    acc[layer % 2, tap, pl.ds(first, count), pl.ds(PAD, cols)] += total
                 else:
-                    acc[tap, pl.ds(first, count), pl.ds(PAD, cols)] = total
+                    acc[layer % 2, tap, pl.ds(first, count), pl.ds(PAD, cols)] = total
             return carry
 
         lax.fori_loop(first_tap, first_tap + taps, across, 0)
-
-    whole_parts = ((0, 1, 1, 3, False), (1, rows - 2, 0, 3, False), (last, 1, 0, 2, False))
-    early_parts = ((0, 1, 2, 3, False), (1, 1, 1, 3, False), (2, rows - 3, 0, 3, False), (last, 1, 0, 2, False))
-    late_parts = ((0, 1, 1, 2, True), (1, 1, 0, 1, True))
 
     def outer(layer, kind):
         @pl.when(has_row[kind])
@@ -230,19 +310,21 @@
             each_piece(layer, kind, range(4), "wait_recv")
             put_halo(layer, kind)
 
-        inner(layer, ((0, 1, 0, 1, True),) if kind == FAR else ((last, 1, 2, 3, True),), 0, 3)
+        inner(layer, ((0, 1, 0, 1, True),) if kind == FAR else ((last, 1, 2, 3, True),), 0, 3, both)
 
     def finish(layer, row):
-        total = acc[0, row, pl.ds(PAD - 1, cols)] + acc[1, row, pl.ds(PAD, cols)]
-        total = jnp.maximum(total + acc[2, row, pl.ds(PAD + 1, cols)], 0.0)
+        part = acc.at[layer % 2, :, row]
+        total = part[0, pl.ds(PAD - 1, cols)] + part[1, pl.ds(PAD, cols)]
+        total = jnp.maximum(total + part[2, pl.ds(PAD + 1, cols)], 0.0)
         if layer == layers - 1:
             out[place(row, rows)] = total
         else:
             mid[layer, row] = total
 
     def blank():
-        acc[:, :, pl.ds(0, PAD)] = jnp.zeros((3, rows, PAD, chans), jnp.float32)
-        acc[:, :, pl.ds(PAD + cols, PAD)] = jnp.zeros((3, rows, PAD, chans), jnp.float32)
+        margin = jnp.zeros((2, 3, rows, PAD, chans), jnp.float32)
+        acc[:, :, :, pl.ds(0, PAD)] = margin
+        acc[:, :, :, pl.ds(PAD + cols, PAD)] = margin
         for kind, spot in ((FAR, 0), (NEAR, rows + 1)):
 
             @pl.when(jnp.logical_not(has_row[kind]))
@@ -258,65 +340,98 @@
                     for kind in range(2):
                         hshift[layer, kind, side] = jnp.zeros((part, LANES), jnp.float32)
 
+    pl.semaphore_wait(barrier, count)
+    start_far(0, 0)
     for load in loads_x:
         load.wait()
-    pack_frames(0, 0)
+    pack_half(0, FAR)
+    start_far(0, 1)
+    each_piece(0, NEAR, range(1), "start")
+    for per_layer in loads_w:
+        for load in per_layer:
+            load.start()
+    for block in (0, 2, 1):
+        pack_frames(0, block)
+        send_frames(0, block)
     pack_half(0, NEAR)
-    pack_half(0, FAR)
+    each_piece(0, NEAR, range(1, 2), "start")
     blank()
-    pl.semaphore_wait(barrier, count)
-    send_frames(0, 0)
-    each_piece(0, NEAR, range(2), "start")
+    for row in range(rows):
+        put_row_upper(0, row)
     split_weights(0)
+    seen = set()
+    parts = parts_of(range(rows), seen)
+    inner(0, parts, 0, 1, both[1:])
     take_frames(0, 0)
+    each_piece(0, FAR, range(2, 4), "start")
+    take_frames(0, 2)
     each_piece(0, NEAR, range(2, 4), "start")
+    inner(0, parts, 1, 2, both[1:])
+    take_frames(0, 1)
     for row in range(rows):
-        put_row(0, row)
-    inner(0, whole_parts, 0, 1)
-    each_piece(0, FAR, range(4), "start")
-    inner(0, whole_parts, 1, 2)
+        put_row_lower(0, row)
+    parts = parts_of(range(rows), seen)
+    forward(0, 0)
+    inner(0, parts, 0, 2, both[:1])
+    forward(0, 1)
+    inner(0, parts, 2, 1, both[:1])
     for layer in range(layers):
         final = layer == layers - 1
+        after = layer + 1
+        for row in range(1, last):
+            finish(layer, row)
+        if not final:
+            pack_frames(after, 1)
+            send_frames(after, 1)
+            split_weights(after)
+        outer(layer, FAR)
+        finish(layer, 0)
+        if not final:
+            start_far(after, 0)
+            pack_half(after, FAR)
+            start_far(after, 1)
+            pack_frames(after, 0)
+            send_frames(after, 0)
         outer(layer, NEAR)
         finish(layer, last)
         if not final:
-            each_piece(layer + 1, NEAR, range(1), "start")
-            pack_frames(layer + 1, 2)
-            send_frames(layer + 1, 2)
-            pack_half(layer + 1, NEAR)
-            each_piece(layer + 1, NEAR, range(1, 2), "start")
-        for row in range(1, last):
-            finish(layer, row)
-        if not final:
-            pack_frames(layer + 1, 1)
-            send_frames(layer + 1, 1)
-            split_weights(layer + 1)
-            take_frames(layer + 1, 2)
-            each_piece(layer + 1, NEAR, range(2, 4), "start")
-            put_row(layer + 1, last)
-            take_frames(layer + 1, 1)
+            each_piece(after, NEAR, range(1), "start")
+            pack_frames(after, 2)
+            send_frames(after, 2)
+            pack_half(after, NEAR)
+            each_piece(after, NEAR, range(1, 2), "start")
+            take_frames(after, 1)
             for row in range(1, last):
-                put_row(layer + 1, row)
-        outer(layer, FAR)
-        finish(layer, 0)
-        if not final:
-            each_piece(layer + 1, FAR, range(1), "start")
-            pack_frames(layer + 1, 0)
-            send_frames(layer + 1, 0)
-            pack_half(layer + 1, FAR)
-            each_piece(layer + 1, FAR, range(1, 2), "start")
-            inner(layer + 1, early_parts, 0, 1)
-            take_frames(layer + 1, 0)
-            each_piece(layer + 1, FAR, range(2, 4), "start")
-            inner(layer + 1, early_parts, 1, 2)
-            put_row(layer + 1, 0)
-            inner(layer + 1, late_parts, 0, 3)
+                put_row_upper(after, row)
+                put_row_lower(after, row)
+            seen = set()
+            parts = parts_of(range(1, last), seen)
+            inner(after, parts, 0, 2, both)
+            take_frames(after, 0)
+            each_piece(after, FAR, range(2, 4), "start")
+            forward(after, 0)
+            inner(after, parts, 2, 1, both)
+            take_frames(after, 2)
+            each_piece(after, NEAR, range(2, 4), "start")
+            put_row_upper(after, 0)
+            put_row_lower(after, 0)
+            inner(after, parts_of((0,), seen), 0, 3, both)
+            forward(after, 1)
+            put_row_upper(after, last)
+            put_row_lower(after, last)
+            inner(after, parts_of((last,), seen), 0, 3, both)
 
     for layer in range(layers):
         for kind in range(2):
             each_piece(layer, kind, range(4), "wait_send")
+        for piece in range(2):
+
+            @pl.when(relays(piece))
+            def _():
+                relay_copy(layer, piece).wait_send()
+
         for side in range(2):
-            for block in range(len(blocks(layer))):
+            for block in range(len(blocks)):
 
                 @pl.when(has_frame[side])
                 def _():
@@ -349,7 +464,7 @@
             pltpu.VMEM(conv_weight.shape, f32),
             pltpu.VMEM((layers, 3, 9 * chans, chans), bf16),
             pltpu.VMEM((rows + 2, cols, 3 * chans), bf16),
-            pltpu.VMEM((3, rows, cols + 2 * PAD, chans), f32),
+            pltpu.VMEM((2, 3, rows, cols + 2 * PAD, chans), f32),
             pltpu.VMEM((layers - 1, rows, cols, chans), f32),
             pltpu.VMEM((layers, 2, rows, part, LANES), f32),
             pltpu.VMEM((layers, 2, rows, part, LANES), f32),
@@ -357,12 +472,16 @@
             pltpu.VMEM((layers, 2, cols, chans - LANES), f32),
             pltpu.VMEM((layers, 2, halved, LANES), f32),
             pltpu.VMEM((layers, 2, 2, part, LANES), f32),
+            pltpu.VMEM((layers, cols, chans - LANES), f32),
+            pltpu.VMEM((layers, halved, LANES), f32),
             dma((rows,)),
             dma((layers, 3)),
             dma((layers, 2, 4)),
             dma((layers, 2, 4)),
             dma((layers, 2, 3)),
             dma((layers, 2, 3)),
+            dma((layers, 2)),
+            dma((layers, 2)),
         ],
         compiler_params=pltpu.CompilerParams(
             collective_id=0, has_side_effects=True, vmem_limit_bytes=62 * 1024 * 1024

time: 32.5 us -> 29.3 us (0.902)
  the two profiles are of different devices: /device:TPU:17 before, /device:TPU:0 now
where the time goes in v2:
time: 29.3 us; the launch traced here: 29.1 us
  Pallas kernels  29.1 us (99%)
    pallas_call x1, Pallas kernels, local(): pl.pallas_call(kernel, out_shape=pltpu.VMEM((rows, cols, chans), f32), in...  28.1 us
    pallas_call x1, Pallas kernels, local(): pl.pallas_call(store, out_shape=jax.ShapeDtypeStruct(features.shape, f32)...  1 us

profile of v2, /device:TPU:0, one launch (start us, length us, event | category | flops | bytes accessed | tf_op | source)
XLA Modules:
  0.0 29.1 jit_solution(15864378526429915598)
XLA Ops:
  0.0 28.1 %shard_map.28.y_ref = f32[4,256,256]{2,1,0:T(8,128)S(1)} custom-call(f32[1,4,256,256]{3,2,1,0:T(8,128)} %x_hbm.1, f32[2,3,3,256,256]{4,3,2,1,0:T(8,128)} %w_hbm.1), custom_call_target="tpu_custom_call" | custom-call | tf_op jit(solution)/shard_map/pallas_call | solution.py:457
  28.1 1.0 %shard_map.29 = f32[1,4,256,256]{3,2,1,0:T(8,128)} custom-call(f32[4,256,256]{2,1,0:T(8,128)S(1)} %shard_map.28.y_ref), custom_call_target="tpu_custom_call" | custom-call | tf_op jit(solution)/shard_map/pallas_call | solution.py:490

commit v3 on v2

--- a/solution.py
+++ b/solution.py
@@ -97,10 +97,7 @@
     def row_copy(layer, kind, piece, relay=False):
         if piece == 0:
             upper = pl.ds(LANES, chans - LANES)
-            if layer == 0:
-                source = x_hbm.at[0, place(edge[kind], rows), :, upper]
-            else:
-                source = maps(layer).at[edge[kind], :, upper]
+            source = maps(layer).at[edge[kind], :, upper]
             target = hmain.at[layer, kind]
         elif piece == 1:
             source, target = half.at[layer, kind], hhalf.at[layer, kind]
@@ -135,8 +132,12 @@
         def _():
             row_copy(layer, FAR, piece).start()
 
-    def forward(layer, piece):
-        @pl.when(relays(piece))
+    def forward(layer, piece, alone=None):
+        chosen = relays(piece)
+        if alone is not None:
+            chosen = chosen & (jnp.logical_not(relays(0)) if alone else relays(0))
+
+        @pl.when(chosen)
         def _():
             row_copy(layer, FAR, piece, True).wait_recv()
             relay_copy(layer, piece).start()
@@ -340,13 +341,17 @@
                     for kind in range(2):
                         hshift[layer, kind, side] = jnp.zeros((part, LANES), jnp.float32)
 
+    for load in loads_x:
+        load.wait()
     pl.semaphore_wait(barrier, count)
     start_far(0, 0)
-    for load in loads_x:
-        load.wait()
     pack_half(0, FAR)
     start_far(0, 1)
-    each_piece(0, NEAR, range(1), "start")
+
+    @pl.when(has_row[NEAR] & jnp.logical_not(relayed(0)))
+    def _():
+        row_copy(0, NEAR, 0).start()
+
     for per_layer in loads_w:
         for load in per_layer:
             load.start()
@@ -354,7 +359,6 @@
         pack_frames(0, block)
         send_frames(0, block)
     pack_half(0, NEAR)
-    each_piece(0, NEAR, range(1, 2), "start")
     blank()
     for row in range(rows):
         put_row_upper(0, row)
@@ -362,10 +366,17 @@
     seen = set()
     parts = parts_of(range(rows), seen)
     inner(0, parts, 0, 1, both[1:])
+
+    @pl.when(has_row[NEAR] & relayed(0))
+    def _():
+        row_copy(0, NEAR, 0).start()
+
+    each_piece(0, NEAR, range(1, 2), "start")
     take_frames(0, 0)
     each_piece(0, FAR, range(2, 4), "start")
     take_frames(0, 2)
     each_piece(0, NEAR, range(2, 4), "start")
+    forward(0, 1, True)
     inner(0, parts, 1, 2, both[1:])
     take_frames(0, 1)
     for row in range(rows):
@@ -373,7 +384,7 @@
     parts = parts_of(range(rows), seen)
     forward(0, 0)
     inner(0, parts, 0, 2, both[:1])
-    forward(0, 1)
+    forward(0, 1, False)
     inner(0, parts, 2, 1, both[:1])
     for layer in range(layers):
         final = layer == layers - 1
@@ -409,6 +420,7 @@
             inner(after, parts, 0, 2, both)
             take_frames(after, 0)
             each_piece(after, FAR, range(2, 4), "start")
+            forward(after, 1, True)
             forward(after, 0)
             inner(after, parts, 2, 1, both)
             take_frames(after, 2)
@@ -416,7 +428,7 @@
             put_row_upper(after, 0)
             put_row_lower(after, 0)
             inner(after, parts_of((0,), seen), 0, 3, both)
-            forward(after, 1)
+            forward(after, 1, False)
             put_row_upper(after, last)
             put_row_lower(after, last)
             inner(after, parts_of((last,), seen), 0, 3, both)

time: 29.3 us -> 28.1 us (0.959)
  the two profiles are of different devices: /device:TPU:0 before, /device:TPU:25 now
where the time goes in v3:
time: 28.1 us; the launch traced here: 27.6 us
  Pallas kernels  27.6 us (98%)
    pallas_call x1, Pallas kernels, local(): pl.pallas_call(kernel, out_shape=pltpu.VMEM((rows, cols, chans), f32), in...  26.6 us
    pallas_call x1, Pallas kernels, local(): pl.pallas_call(store, out_shape=jax.ShapeDtypeStruct(features.shape, f32)...  1 us

profile of v3, /device:TPU:25, one launch (start us, length us, event | category | flops | bytes accessed | tf_op | source)
XLA Modules:
  0.0 27.6 jit_solution(9377940511968657781)
XLA Ops:
  0.0 26.6 %shard_map.28.y_ref = f32[4,256,256]{2,1,0:T(8,128)S(1)} custom-call(f32[1,4,256,256]{3,2,1,0:T(8,128)} %x_hbm.1, f32[2,3,3,256,256]{4,3,2,1,0:T(8,128)} %w_hbm.1), custom_call_target="tpu_custom_call" | custom-call | tf_op jit(solution)/shard_map/pallas_call | solution.py:469
  26.6 1.0 %shard_map.29 = f32[1,4,256,256]{3,2,1,0:T(8,128)} custom-call(f32[4,256,256]{2,1,0:T(8,128)S(1)} %shard_map.28.y_ref), custom_call_target="tpu_custom_call" | custom-call | tf_op jit(solution)/shard_map/pallas_call | solution.py:502

commit v4 on v2

--- a/solution.py
+++ b/solution.py
@@ -48,8 +48,7 @@
         return 4 * (step + (place % 2) * (pairs - 1 - 2 * step)) // pairs
 
     def takes(place, piece):
-        quarters = shared(place)
-        return quarters >= 2 if piece == 0 else quarters % 2 == 1
+        return shared(place) > piece
 
     def within(place):
         return (place >= 0) & (place < bands)
@@ -66,9 +65,9 @@
     def place(row, count):
         return row + turned * (count - 1 - 2 * row)
 
-    loads_x = [pltpu.make_async_copy(x_hbm.at[0, place(q, rows)], xin.at[q], load_x.at[q]) for q in range(rows)]
+    loads_x = [pltpu.make_async_copy(x_hbm.at[0, place(q, rows)], xin.at[q], load_x) for q in range(rows)]
     loads_w = [
-        [pltpu.make_async_copy(w_hbm.at[n, place(d, 3)], wbuf.at[n, d], load_w.at[n, d]) for d in range(3)]
+        [pltpu.make_async_copy(w_hbm.at[n, place(d, 3)], wbuf.at[n, d], load_w.at[n]) for d in range(3)]
         for n in range(layers)
     ]
     for load in loads_x:
@@ -94,33 +93,37 @@
     def maps(layer):
         return xin if layer == 0 else mid.at[layer - 1]
 
+    def section(piece):
+        return pl.ds(piece * (cols // 2), cols // 2)
+
     def row_copy(layer, kind, piece, relay=False):
-        if piece == 0:
-            upper = pl.ds(LANES, chans - LANES)
-            if layer == 0:
-                source = x_hbm.at[0, place(edge[kind], rows), :, upper]
-            else:
-                source = maps(layer).at[edge[kind], :, upper]
-            target = hmain.at[layer, kind]
-        elif piece == 1:
-            source, target = half.at[layer, kind], hhalf.at[layer, kind]
+        if piece < 2:
+            source = maps(layer).at[edge[kind], section(piece), pl.ds(LANES, chans - LANES)]
+            target = (rmain.at[layer] if relay else hmain.at[layer, kind]).at[section(piece)]
+        elif piece == 2:
+            source = half.at[layer, kind]
+            target = rhalf.at[layer] if relay else hhalf.at[layer, kind]
         else:
-            source = got.at[layer, piece - 2, edge[kind]]
-            target = hshift.at[layer, kind, piece - 2]
+            source = got.at[layer, piece - 3, edge[kind]]
+            target = hshift.at[layer, kind, piece - 3]
         return pltpu.make_async_remote_copy(
             src_ref=source,
-            dst_ref=(rmain, rhalf)[piece].at[layer] if relay else target,
-            send_sem=row_send.at[layer, kind, piece],
+            dst_ref=target,
+            send_sem=row_send.at[kind, piece],
             recv_sem=relay_recv.at[layer, piece] if relay else row_recv.at[layer, kind, piece],
             device_id={"row": row_to[NEAR if relay else kind]},
             device_id_type=MESH,
         )
 
     def relay_copy(layer, piece):
+        if piece < 2:
+            source, target = (ref.at[section(piece)] for ref in (rmain.at[layer], hmain.at[layer, FAR]))
+        else:
+            source, target = rhalf.at[layer], hhalf.at[layer, FAR]
         return pltpu.make_async_remote_copy(
-            src_ref=(rmain, rhalf)[piece].at[layer],
-            dst_ref=(hmain, hhalf)[piece].at[layer, FAR],
-            send_sem=relay_send.at[layer, piece],
+            src_ref=source,
+            dst_ref=target,
+            send_sem=relay_send.at[piece],
             recv_sem=row_recv.at[layer, FAR, piece],
             device_id={"row": onward},
             device_id_type=MESH,
@@ -134,6 +137,31 @@
         @pl.when(has_row[FAR] & jnp.logical_not(relayed(piece)))
         def _():
             row_copy(layer, FAR, piece).start()
+
+    def drain_frames(layer, block):
+        for side in range(2):
+
+            @pl.when(has_frame[side])
+            def _():
+                frame_copy(layer, side, block).wait_send()
+
+    def drain(layer):
+        for kind in range(2):
+            each_piece(layer, kind, range(5), "wait_send")
+        for piece in range(3):
+
+            @pl.when(relays(piece))
+            def _():
+                relay_copy(layer, piece).wait_send()
+
+        for block in range(len(blocks)):
+            drain_frames(layer, block)
+
+    def start_near(layer, late):
+        @pl.when(has_row[NEAR] & (relayed(1) if late else jnp.logical_not(relayed(1))))
+        def _():
+            for piece in range(3):
+                row_copy(layer, NEAR, piece).start()
 
     def forward(layer, piece):
         @pl.when(relays(piece))
@@ -142,7 +170,7 @@
             relay_copy(layer, piece).start()
 
     def sent(kind, piece):
-        return has_row[kind] if piece < 2 else has_row[kind] & has_frame[3 - piece]
+        return has_row[kind] if piece < 3 else has_row[kind] & has_frame[4 - piece]
 
     def each_piece(layer, kind, pieces, action):
         for piece in pieces:
@@ -158,7 +186,7 @@
         return pltpu.make_async_remote_copy(
             src_ref=pack.at[layer, side, pl.ds(start, size)],
             dst_ref=got.at[layer, side, pl.ds(start, size)],
-            send_sem=frame_send.at[layer, side, block],
+            send_sem=frame_send.at[side, block],
             recv_sem=frame_recv.at[layer, side, block],
             device_id={"frame": frame_to[side]},
             device_id_type=MESH,
@@ -243,11 +271,9 @@
             return pltpu.roll(value, shift, 1) if shift else value
 
         put_lower(spot, rest_of, lambda side: hshift[layer, kind, side])
-        put_upper(spot, hmain.at[layer, kind])
 
     def split_weights(layer):
-        for load in loads_w[layer]:
-            load.wait()
+        pltpu.make_async_copy(w_hbm.at[layer], wbuf.at[layer], load_w.at[layer]).wait()
 
         def tap(index, carry):
             down, across = index // 3, index % 3
@@ -305,12 +331,21 @@
         lax.fori_loop(first_tap, first_tap + taps, across, 0)
 
     def outer(layer, kind):
-        @pl.when(has_row[kind])
-        def _():
-            each_piece(layer, kind, range(4), "wait_recv")
-            put_halo(layer, kind)
-
-        inner(layer, ((0, 1, 0, 1, True),) if kind == FAR else ((last, 1, 2, 3, True),), 0, 3, both)
+        spot = 0 if kind == FAR else rows + 1
+        parts = ((0, 1, 0, 1, True),) if kind == FAR else ((last, 1, 2, 3, True),)
+        steps = (both[1:], both[:1]) if layer == layers - 1 and kind == NEAR else (both,)
+        for step in steps:
+
+            @pl.when(has_row[kind])
+            def _():
+                if 1 in step:
+                    each_piece(layer, kind, range(2), "wait_recv")
+                    put_upper(spot, hmain.at[layer, kind])
+                if 0 in step:
+                    each_piece(layer, kind, range(2, 5), "wait_recv")
+                    put_halo(layer, kind)
+
+            inner(layer, parts, 0, 3, step)
 
     def finish(layer, row):
         part = acc.at[layer % 2, :, row]
@@ -340,13 +375,12 @@
                     for kind in range(2):
                         hshift[layer, kind, side] = jnp.zeros((part, LANES), jnp.float32)
 
+    pltpu.make_async_copy(x_hbm.at[0], xin, load_x).wait()
     pl.semaphore_wait(barrier, count)
     start_far(0, 0)
-    for load in loads_x:
-        load.wait()
+    start_far(0, 1)
     pack_half(0, FAR)
-    start_far(0, 1)
-    each_piece(0, NEAR, range(1), "start")
+    start_far(0, 2)
     for per_layer in loads_w:
         for load in per_layer:
             load.start()
@@ -354,7 +388,7 @@
         pack_frames(0, block)
         send_frames(0, block)
     pack_half(0, NEAR)
-    each_piece(0, NEAR, range(1, 2), "start")
+    start_near(0, False)
     blank()
     for row in range(rows):
         put_row_upper(0, row)
@@ -362,18 +396,21 @@
     seen = set()
     parts = parts_of(range(rows), seen)
     inner(0, parts, 0, 1, both[1:])
+    start_near(0, True)
     take_frames(0, 0)
-    each_piece(0, FAR, range(2, 4), "start")
+    each_piece(0, FAR, range(3, 5), "start")
     take_frames(0, 2)
-    each_piece(0, NEAR, range(2, 4), "start")
-    inner(0, parts, 1, 2, both[1:])
+    each_piece(0, NEAR, range(3, 5), "start")
+    inner(0, parts, 1, 1, both[1:])
+    forward(0, 0)
+    inner(0, parts, 2, 1, both[1:])
     take_frames(0, 1)
     for row in range(rows):
         put_row_lower(0, row)
     parts = parts_of(range(rows), seen)
-    forward(0, 0)
+    forward(0, 1)
     inner(0, parts, 0, 2, both[:1])
-    forward(0, 1)
+    forward(0, 2)
     inner(0, parts, 2, 1, both[:1])
     for layer in range(layers):
         final = layer == layers - 1
@@ -382,24 +419,30 @@
             finish(layer, row)
         if not final:
             pack_frames(after, 1)
+            drain_frames(layer, 1)
             send_frames(after, 1)
             split_weights(after)
         outer(layer, FAR)
         finish(layer, 0)
         if not final:
+            each_piece(layer, FAR, range(5), "wait_send")
             start_far(after, 0)
+            start_far(after, 1)
             pack_half(after, FAR)
-            start_far(after, 1)
+            start_far(after, 2)
             pack_frames(after, 0)
+            drain_frames(layer, 0)
             send_frames(after, 0)
         outer(layer, NEAR)
         finish(layer, last)
         if not final:
-            each_piece(after, NEAR, range(1), "start")
+            each_piece(layer, NEAR, range(5), "wait_send")
+            each_piece(after, NEAR, range(2), "start")
             pack_frames(after, 2)
+            drain_frames(layer, 2)
             send_frames(after, 2)
             pack_half(after, NEAR)
-            each_piece(after, NEAR, range(1, 2), "start")
+            each_piece(after, NEAR, range(2, 3), "start")
             take_frames(after, 1)
             for row in range(1, last):
                 put_row_upper(after, row)
@@ -407,35 +450,28 @@
             seen = set()
             parts = parts_of(range(1, last), seen)
             inner(after, parts, 0, 2, both)
+            for piece in range(3):
+
+                @pl.when(relays(piece))
+                def _():
+                    relay_copy(layer, piece).wait_send()
+
             take_frames(after, 0)
-            each_piece(after, FAR, range(2, 4), "start")
+            each_piece(after, FAR, range(3, 5), "start")
             forward(after, 0)
             inner(after, parts, 2, 1, both)
             take_frames(after, 2)
-            each_piece(after, NEAR, range(2, 4), "start")
+            each_piece(after, NEAR, range(3, 5), "start")
+            forward(after, 1)
             put_row_upper(after, 0)
             put_row_lower(after, 0)
             inner(after, parts_of((0,), seen), 0, 3, both)
-            forward(after, 1)
+            forward(after, 2)
             put_row_upper(after, last)
             put_row_lower(after, last)
             inner(after, parts_of((last,), seen), 0, 3, both)
 
-    for layer in range(layers):
-        for kind in range(2):
-            each_piece(layer, kind, range(4), "wait_send")
-        for piece in range(2):
-
-            @pl.when(relays(piece))
-            def _():
-                relay_copy(layer, piece).wait_send()
-
-        for side in range(2):
-            for block in range(len(blocks)):
-
-                @pl.when(has_frame[side])
-                def _():
-                    frame_copy(layer, side, block).wait_send()
+    drain(layers - 1)
 
 
 def store(y_ref, o_hbm, sem):
@@ -474,14 +510,14 @@
             pltpu.VMEM((layers, 2, 2, part, LANES), f32),
             pltpu.VMEM((layers, cols, chans - LANES), f32),
             pltpu.VMEM((layers, halved, LANES), f32),
-            dma((rows,)),
+            dma,
+            dma((layers,)),
+            dma((2, 5)),
+            dma((layers, 2, 5)),
+            dma((2, 3)),
+            dma((layers, 2, 3)),
+            dma((3,)),
             dma((layers, 3)),
-            dma((layers, 2, 4)),
-            dma((layers, 2, 4)),
-            dma((layers, 2, 3)),
-            dma((layers, 2, 3)),
-            dma((layers, 2)),
-            dma((layers, 2)),
         ],
         compiler_params=pltpu.CompilerParams(
             collective_id=0, has_side_effects=True, vmem_limit_bytes=62 * 1024 * 1024

time: 29.3 us -> 27.8 us (0.949)
  the two profiles are of different devices: /device:TPU:0 before, /device:TPU:25 now
where the time goes in v4:
time: 27.8 us; the launch traced here: 27.2 us
  Pallas kernels  27.2 us (98%)
    pallas_call x1, Pallas kernels, local(): pl.pallas_call(kernel, out_shape=pltpu.VMEM((rows, cols, chans), f32), in...  26.2 us
    pallas_call x1, Pallas kernels, local(): pl.pallas_call(store, out_shape=jax.ShapeDtypeStruct(features.shape, f32)...  1 us

profile of v4, /device:TPU:25, one launch (start us, length us, event | category | flops | bytes accessed | tf_op | source)
XLA Modules:
  0.0 27.2 jit_solution(2114786299516670734)
XLA Ops:
  0.0 26.2 %shard_map.28.y_ref = f32[4,256,256]{2,1,0:T(8,128)S(1)} custom-call(f32[1,4,256,256]{3,2,1,0:T(8,128)} %x_hbm.1, f32[2,3,3,256,256]{4,3,2,1,0:T(8,128)} %w_hbm.1), custom_call_target="tpu_custom_call" | custom-call | tf_op jit(solution)/shard_map/pallas_call | solution.py:493
  26.2 1.0 %shard_map.29 = f32[1,4,256,256]{3,2,1,0:T(8,128)} custom-call(f32[4,256,256]{2,1,0:T(8,128)S(1)} %shard_map.28.y_ref), custom_call_target="tpu_custom_call" | custom-call | tf_op jit(solution)/shard_map/pallas_call | solution.py:526

commit v5 on v4

--- a/solution.py
+++ b/solution.py
@@ -18,7 +18,7 @@
 
 
 def kernel(
-    x_hbm, w_hbm, out, xin, wbuf, w3, sx, acc, mid, pack, got, half, hmain, hhalf, hshift, rmain, rhalf,
+    x_hbm, w_hbm, out, w3, sx, acc, xin, wbuf, mid, pack, got, half, hmain, hhalf, hshift, rmain, rhalf,
     load_x, load_w, row_send, row_recv, frame_send, frame_recv, relay_send, relay_recv,
 ):
     rows, cols, chans = xin.shape
@@ -345,7 +345,8 @@
                     each_piece(layer, kind, range(2, 5), "wait_recv")
                     put_halo(layer, kind)
 
-            inner(layer, parts, 0, 3, step)
+            if steps == (both,) or 0 not in step:
+                inner(layer, parts, 0, 3, step)
 
     def finish(layer, row):
         part = acc.at[layer % 2, :, row]
@@ -434,8 +435,8 @@
             drain_frames(layer, 0)
             send_frames(after, 0)
         outer(layer, NEAR)
-        finish(layer, last)
         if not final:
+            finish(layer, last)
             each_piece(layer, NEAR, range(5), "wait_send")
             each_piece(after, NEAR, range(2), "start")
             pack_frames(after, 2)
@@ -474,10 +475,43 @@
     drain(layers - 1)
 
 
-def store(y_ref, o_hbm, sem):
-    copies = [pltpu.make_async_copy(y_ref.at[n], o_hbm.at[0, n], sem.at[n]) for n in range(y_ref.shape[0])]
+def store(y_ref, w3, sx, acc, o_hbm, total, ready, sem):
+    rows, cols, chans = y_ref.shape
+    layers = w3.shape[0]
+    last = rows - 1
+    deep = 3 * LANES
+    turned = lax.axis_index("row") % 2
+
+    def place(row):
+        return row + turned * (last - 2 * row)
+
+    copies = [
+        pltpu.make_async_copy(y_ref.at[place(row)], o_hbm.at[0, place(row)], sem.at[row]) for row in range(last)
+    ]
     for copy in copies:
         copy.start()
+    margin = jnp.zeros((3, PAD, chans), jnp.float32)
+    total[:, pl.ds(0, PAD)] = margin
+    total[:, pl.ds(PAD + cols, PAD)] = margin
+    middle = cols // 2
+    cuts = ((0, middle + 2 * PAD, 0, middle), (middle + 2 * PAD, cols, middle, cols))
+    for n, (start, stop, begin, end) in enumerate(cuts):
+        for tap in range(3):
+            extra = jnp.dot(
+                sx[rows + 1, pl.ds(start, stop - start), pl.ds(0, deep)],
+                w3[layers - 1, tap, pl.ds(2 * deep, deep)],
+                preferred_element_type=jnp.float32,
+            )
+            here = pl.ds(PAD + start, stop - start)
+            total[tap, here] = acc[(layers - 1) % 2, tap, last, here] + extra
+        size = end - begin
+        value = total[0, pl.ds(PAD + begin - 1, size)] + total[1, pl.ds(PAD + begin, size)]
+        ready[pl.ds(begin, size)] = jnp.maximum(value + total[2, pl.ds(PAD + begin + 1, size)], 0.0)
+        copy = pltpu.make_async_copy(
+            ready.at[pl.ds(begin, size)], o_hbm.at[0, place(last), pl.ds(begin, size)], sem.at[last + n]
+        )
+        copy.start()
+        copies.append(copy)
     for copy in copies:
         copy.wait()
 
@@ -490,17 +524,19 @@
     halved = cols // (LANES // (LANES - 2 * fold))
     f32, bf16 = jnp.float32, jnp.bfloat16
     dma = pltpu.SemaphoreType.DMA
-    result = pl.pallas_call(
+    results = pl.pallas_call(
         kernel,
-        out_shape=pltpu.VMEM((rows, cols, chans), f32),
+        out_shape=(
+            pltpu.VMEM((rows, cols, chans), f32),
+            pltpu.VMEM((layers, 3, 9 * chans, chans), bf16),
+            pltpu.VMEM((rows + 2, cols, 3 * chans), bf16),
+            pltpu.VMEM((2, 3, rows, cols + 2 * PAD, chans), f32),
+        ),
         in_specs=[pl.BlockSpec(memory_space=pl.ANY)] * 2,
-        out_specs=pl.BlockSpec(memory_space=pltpu.VMEM),
+        out_specs=(pl.BlockSpec(memory_space=pltpu.VMEM),) * 4,
         scratch_shapes=[
             pltpu.VMEM((rows, cols, chans), f32),
             pltpu.VMEM(conv_weight.shape, f32),
-            pltpu.VMEM((layers, 3, 9 * chans, chans), bf16),
-            pltpu.VMEM((rows + 2, cols, 3 * chans), bf16),
-            pltpu.VMEM((2, 3, rows, cols + 2 * PAD, chans), f32),
             pltpu.VMEM((layers - 1, rows, cols, chans), f32),
             pltpu.VMEM((layers, 2, rows, part, LANES), f32),
             pltpu.VMEM((layers, 2, rows, part, LANES), f32),
@@ -520,17 +556,21 @@
             dma((layers, 3)),
         ],
         compiler_params=pltpu.CompilerParams(
-            collective_id=0, has_side_effects=True, vmem_limit_bytes=62 * 1024 * 1024
+            collective_id=0, has_side_effects=True, vmem_limit_bytes=47 * 1024 * 1024
         ),
     )(features, conv_weight)
     return pl.pallas_call(
         store,
         out_shape=jax.ShapeDtypeStruct(features.shape, f32),
-        in_specs=[pl.BlockSpec(memory_space=pltpu.VMEM)],
+        in_specs=[pl.BlockSpec(memory_space=pltpu.VMEM)] * 4,
         out_specs=pl.BlockSpec(memory_space=pl.ANY),
-        scratch_shapes=[dma((rows,))],
-        compiler_params=pltpu.CompilerParams(vmem_limit_bytes=2 * 1024 * 1024),
-    )(result)
+        scratch_shapes=[
+            pltpu.VMEM((3, cols + 2 * PAD, chans), f32),
+            pltpu.VMEM((cols, chans), f32),
+            dma((rows + 1,)),
+        ],
+        compiler_params=pltpu.CompilerParams(vmem_limit_bytes=4 * 1024 * 1024),
+    )(*results)
 
 
 def solution(mesh):

time: 27.8 us -> 27.3 us (0.982)
  Pallas kernels: 27.2 us -> 26.7 us
    pallas_call x1, Pallas kernels: 26.2 us -> 25.5 us  [local(): pl.pallas_call(kernel, out_shape=(pltpu.VMEM((rows, cols, chans), f32), p...]
where the time goes in v5:
time: 27.3 us; the launch traced here: 26.7 us
  Pallas kernels  26.7 us (98%)
    pallas_call x1, Pallas kernels, local(): pl.pallas_call(kernel, out_shape=(pltpu.VMEM((rows, cols, chans), f32), p...  25.5 us
    pallas_call x1, Pallas kernels, local(): pl.pallas_call(store, out_shape=jax.ShapeDtypeStruct(features.shape, f32)...  1.25 us

profile of v5, /device:TPU:25, one launch (start us, length us, event | category | flops | bytes accessed | tf_op | source)
XLA Modules:
  0.0 26.7 jit_solution(1237213074383212742)
XLA Ops:
  0.0 25.5 %shard_map.28 = (f32[4,256,256]{2,1,0:T(8,128)S(1)}, bf16[2,3,2304,256]{3,2,1,0:T(8,128)(2,1)S(1)}, bf16[6,256,768]{2,1,0:T(8,128)(2,1)S(1)}, f32[2,3,4,272,256]{4,3,2,1,0:T(8,128)S(1)}) custom-call(f32[1,4,256,256]{3,2,1,0:T(8,128)} %x_hbm.1, f32[2,3,3,256,256]{4,3,2,1,0:T(8,128)} %w_hbm.1), custom_call_target="tpu_custom_call" | custom-call | tf_op jit(solution)/shard_map/pallas_call | solution.py:527
  25.5 1.3 %shard_map.29 = f32[1,4,256,256]{3,2,1,0:T(8,128)} custom-call(f32[4,256,256]{2,1,0:T(8,128)S(1)} %get-tuple-element.9.y_ref, bf16[2,3,2304,256]{3,2,1,0:T(8,128)(2,1)S(1)} %get-tuple-element.10.w3, bf16[6,256,768]{2,1,0:T(8,128)(2,1)S(1)} %get-tuple-element.11.sx, f32[2,3,4,272,256]{4,3,2,1,0:T(8,128)S(1)} %get-tuple-element.12.acc), custom_call_target="tpu_custom_call" | custom-call | tf_op jit(solution)/shard_map/pallas_call | solution.py:562

commit v6 on v5

--- a/solution.py
+++ b/solution.py
@@ -377,18 +377,19 @@
                         hshift[layer, kind, side] = jnp.zeros((part, LANES), jnp.float32)
 
     pltpu.make_async_copy(x_hbm.at[0], xin, load_x).wait()
-    pl.semaphore_wait(barrier, count)
-    start_far(0, 0)
-    start_far(0, 1)
-    pack_half(0, FAR)
-    start_far(0, 2)
     for per_layer in loads_w:
         for load in per_layer:
             load.start()
+    pack_half(0, FAR)
     for block in (0, 2, 1):
         pack_frames(0, block)
-        send_frames(0, block)
     pack_half(0, NEAR)
+    pl.semaphore_wait(barrier, count)
+    send_frames(0, 0)
+    send_frames(0, 2)
+    for piece in range(3):
+        start_far(0, piece)
+    send_frames(0, 1)
     start_near(0, False)
     blank()
     for row in range(rows):

time: 27.3 us -> 27.1 us (level)
  no operation moved by 1% of the time
where the time goes in v6:
time: 27.1 us; the launch traced here: 26.7 us
  Pallas kernels  26.7 us (99%)
    pallas_call x1, Pallas kernels, local(): pl.pallas_call(kernel, out_shape=(pltpu.VMEM((rows, cols, chans), f32), p...  25.4 us
    pallas_call x1, Pallas kernels, local(): pl.pallas_call(store, out_shape=jax.ShapeDtypeStruct(features.shape, f32)...  1.26 us

profile of v6, /device:TPU:25, one launch (start us, length us, event | category | flops | bytes accessed | tf_op | source)
XLA Modules:
  0.0 26.7 jit_solution(12889241809066008919)
XLA Ops:
  0.0 25.4 %shard_map.28 = (f32[4,256,256]{2,1,0:T(8,128)S(1)}, bf16[2,3,2304,256]{3,2,1,0:T(8,128)(2,1)S(1)}, bf16[6,256,768]{2,1,0:T(8,128)(2,1)S(1)}, f32[2,3,4,272,256]{4,3,2,1,0:T(8,128)S(1)}) custom-call(f32[1,4,256,256]{3,2,1,0:T(8,128)} %x_hbm.1, f32[2,3,3,256,256]{4,3,2,1,0:T(8,128)} %w_hbm.1), custom_call_target="tpu_custom_call" | custom-call | tf_op jit(solution)/shard_map/pallas_call | solution.py:528
  25.4 1.3 %shard_map.29 = f32[1,4,256,256]{3,2,1,0:T(8,128)} custom-call(f32[4,256,256]{2,1,0:T(8,128)S(1)} %get-tuple-element.9.y_ref, bf16[2,3,2304,256]{3,2,1,0:T(8,128)(2,1)S(1)} %get-tuple-element.10.w3, bf16[6,256,768]{2,1,0:T(8,128)(2,1)S(1)} %get-tuple-element.11.sx, f32[2,3,4,272,256]{4,3,2,1,0:T(8,128)S(1)} %get-tuple-element.12.acc), custom_call_target="tpu_custom_call" | custom-call | tf_op jit(solution)/shard_map/pallas_call | solution.py:563

commit v7 on v6

--- a/solution.py
+++ b/solution.py
@@ -171,6 +171,8 @@
 
     def sent(kind, piece):
         return has_row[kind] if piece < 3 else has_row[kind] & has_frame[4 - piece]
+
+    prompt = has_row[FAR] & (shared(row_to[FAR]) <= 1)
 
     def each_piece(layer, kind, pieces, action):
         for piece in pieces:
@@ -423,7 +425,11 @@
             pack_frames(after, 1)
             drain_frames(layer, 1)
             send_frames(after, 1)
-            split_weights(after)
+
+            @pl.when(jnp.logical_not(prompt))
+            def _():
+                split_weights(after)
+
         outer(layer, FAR)
         finish(layer, 0)
         if not final:
@@ -435,6 +441,11 @@
             pack_frames(after, 0)
             drain_frames(layer, 0)
             send_frames(after, 0)
+
+            @pl.when(prompt)
+            def _():
+                split_weights(after)
+
         outer(layer, NEAR)
         if not final:
             finish(layer, last)

time: 27.1 us -> 26.8 us (0.989); the launches traced: 26.7 us -> 26.7 us
  no operation moved by 1% of the time
where the time goes in v7:
time: 26.8 us; the launch traced here: 26.7 us
  Pallas kernels  26.7 us (100%)
    pallas_call x1, Pallas kernels, local(): pl.pallas_call(kernel, out_shape=(pltpu.VMEM((rows, cols, chans), f32), p...  25.4 us
    pallas_call x1, Pallas kernels, local(): pl.pallas_call(store, out_shape=jax.ShapeDtypeStruct(features.shape, f32)...  1.26 us

profile of v7, /device:TPU:25, one launch (start us, length us, event | category | flops | bytes accessed | tf_op | source)
XLA Modules:
  0.0 26.7 jit_solution(1560948741845145395)
XLA Ops:
  0.0 25.4 %shard_map.28 = (f32[4,256,256]{2,1,0:T(8,128)S(1)}, bf16[2,3,2304,256]{3,2,1,0:T(8,128)(2,1)S(1)}, bf16[6,256,768]{2,1,0:T(8,128)(2,1)S(1)}, f32[2,3,4,272,256]{4,3,2,1,0:T(8,128)S(1)}) custom-call(f32[1,4,256,256]{3,2,1,0:T(8,128)} %x_hbm.1, f32[2,3,3,256,256]{4,3,2,1,0:T(8,128)} %w_hbm.1), custom_call_target="tpu_custom_call" | custom-call | tf_op jit(solution)/shard_map/pallas_call | solution.py:539
  25.4 1.3 %shard_map.29 = f32[1,4,256,256]{3,2,1,0:T(8,128)} custom-call(f32[4,256,256]{2,1,0:T(8,128)S(1)} %get-tuple-element.9.y_ref, bf16[2,3,2304,256]{3,2,1,0:T(8,128)(2,1)S(1)} %get-tuple-element.10.w3, bf16[6,256,768]{2,1,0:T(8,128)(2,1)S(1)} %get-tuple-element.11.sx, f32[2,3,4,272,256]{4,3,2,1,0:T(8,128)S(1)} %get-tuple-element.12.acc), custom_call_target="tpu_custom_call" | custom-call | tf_op jit(solution)/shard_map/pallas_call | solution.py:574

commit v8 on v7

--- a/solution.py
+++ b/solution.py
@@ -450,19 +450,20 @@
         if not final:
             finish(layer, last)
             each_piece(layer, NEAR, range(5), "wait_send")
-            each_piece(after, NEAR, range(2), "start")
             pack_frames(after, 2)
             drain_frames(layer, 2)
             send_frames(after, 2)
             pack_half(after, NEAR)
-            each_piece(after, NEAR, range(2, 3), "start")
+            start_near(after, False)
             take_frames(after, 1)
             for row in range(1, last):
                 put_row_upper(after, row)
                 put_row_lower(after, row)
             seen = set()
             parts = parts_of(range(1, last), seen)
-            inner(after, parts, 0, 2, both)
+            inner(after, parts, 0, 1, both)
+            start_near(after, True)
+            inner(after, parts, 1, 1, both)
             for piece in range(3):
 
                 @pl.when(relays(piece))

time: 26.8 us -> 26.8 us (level)
  no operation moved by 1% of the time
where the time goes in v8:
time: 26.8 us; the launch traced here: 26.7 us
  Pallas kernels  26.7 us (100%)
    pallas_call x1, Pallas kernels, local(): pl.pallas_call(kernel, out_shape=(pltpu.VMEM((rows, cols, chans), f32), p...  25.4 us
    pallas_call x1, Pallas kernels, local(): pl.pallas_call(store, out_shape=jax.ShapeDtypeStruct(features.shape, f32)...  1.25 us

profile of v8, /device:TPU:25, one launch (start us, length us, event | category | flops | bytes accessed | tf_op | source)
XLA Modules:
  0.0 26.7 jit_solution(16083872473444300109)
XLA Ops:
  0.0 25.4 %shard_map.28 = (f32[4,256,256]{2,1,0:T(8,128)S(1)}, bf16[2,3,2304,256]{3,2,1,0:T(8,128)(2,1)S(1)}, bf16[6,256,768]{2,1,0:T(8,128)(2,1)S(1)}, f32[2,3,4,272,256]{4,3,2,1,0:T(8,128)S(1)}) custom-call(f32[1,4,256,256]{3,2,1,0:T(8,128)} %x_hbm.1, f32[2,3,3,256,256]{4,3,2,1,0:T(8,128)} %w_hbm.1), custom_call_target="tpu_custom_call" | custom-call | tf_op jit(solution)/shard_map/pallas_call | solution.py:540
  25.4 1.3 %shard_map.29 = f32[1,4,256,256]{3,2,1,0:T(8,128)} custom-call(f32[4,256,256]{2,1,0:T(8,128)S(1)} %get-tuple-element.9.y_ref, bf16[2,3,2304,256]{3,2,1,0:T(8,128)(2,1)S(1)} %get-tuple-element.10.w3, bf16[6,256,768]{2,1,0:T(8,128)(2,1)S(1)} %get-tuple-element.11.sx, f32[2,3,4,272,256]{4,3,2,1,0:T(8,128)S(1)} %get-tuple-element.12.acc), custom_call_target="tpu_custom_call" | custom-call | tf_op jit(solution)/shard_map/pallas_call | solution.py:575

commit v9 on v8

--- a/solution.py
+++ b/solution.py
@@ -463,7 +463,6 @@
             parts = parts_of(range(1, last), seen)
             inner(after, parts, 0, 1, both)
             start_near(after, True)
-            inner(after, parts, 1, 1, both)
             for piece in range(3):
 
                 @pl.when(relays(piece))
@@ -473,7 +472,7 @@
             take_frames(after, 0)
             each_piece(after, FAR, range(3, 5), "start")
             forward(after, 0)
-            inner(after, parts, 2, 1, both)
+            inner(after, parts, 1, 2, both)
             take_frames(after, 2)
             each_piece(after, NEAR, range(3, 5), "start")
             forward(after, 1)

time: 26.8 us -> 26.8 us (level)
  no operation moved by 1% of the time
where the time goes in v9:
time: 26.8 us; the launch traced here: 26.7 us
  Pallas kernels  26.7 us (100%)
    pallas_call x1, Pallas kernels, local(): pl.pallas_call(kernel, out_shape=(pltpu.VMEM((rows, cols, chans), f32), p...  25.4 us
    pallas_call x1, Pallas kernels, local(): pl.pallas_call(store, out_shape=jax.ShapeDtypeStruct(features.shape, f32)...  1.26 us

profile of v9, /device:TPU:25, one launch (start us, length us, event | category | flops | bytes accessed | tf_op | source)
XLA Modules:
  0.0 26.7 jit_solution(1442143441733464768)
XLA Ops:
  0.0 25.4 %shard_map.28 = (f32[4,256,256]{2,1,0:T(8,128)S(1)}, bf16[2,3,2304,256]{3,2,1,0:T(8,128)(2,1)S(1)}, bf16[6,256,768]{2,1,0:T(8,128)(2,1)S(1)}, f32[2,3,4,272,256]{4,3,2,1,0:T(8,128)S(1)}) custom-call(f32[1,4,256,256]{3,2,1,0:T(8,128)} %x_hbm.1, f32[2,3,3,256,256]{4,3,2,1,0:T(8,128)} %w_hbm.1), custom_call_target="tpu_custom_call" | custom-call | tf_op jit(solution)/shard_map/pallas_call | solution.py:539
  25.4 1.3 %shard_map.29 = f32[1,4,256,256]{3,2,1,0:T(8,128)} custom-call(f32[4,256,256]{2,1,0:T(8,128)S(1)} %get-tuple-element.9.y_ref, bf16[2,3,2304,256]{3,2,1,0:T(8,128)(2,1)S(1)} %get-tuple-element.10.w3, bf16[6,256,768]{2,1,0:T(8,128)(2,1)S(1)} %get-tuple-element.11.sx, f32[2,3,4,272,256]{4,3,2,1,0:T(8,128)S(1)} %get-tuple-element.12.acc), custom_call_target="tpu_custom_call" | custom-call | tf_op jit(solution)/shard_map/pallas_call | solution.py:574
